TPU v7x, 32 devices: a whole 2x2x4 slice. The times are simulated.
32 devices in a mesh: dp: 8 (over y, x, core), mp: 4 (over z).
Axes of the slice: x: 2, y: 2, z: 4, core: 2. Of those that a mesh axis runs over, the one named last changes fastest.
Arguments:
- hidden: bfloat16 [16384, 13824], P('dp', 'mp'), may hold values from -6 to 6
- out_grad: bfloat16 [16384, 5120], P('dp', 'mp'), may hold values from -6 to 6
- proj_in: bfloat16 [64, 13824], P(None, 'mp'), may hold values from -0.0546875 to 0.0546875
- proj_out: bfloat16 [64, 5120], P(None, 'mp'), may hold values from -0.078125 to 0.078125
- segment_ids: int32 [8, 2048], P('dp'), may hold values from 0 to 15, never falling along the last dimension, each value on 1 to 1024 neighbouring positions
Outputs:
- features: float32 [128, 4096], P('dp')
- gram: float32 [4096, 4096], P(('dp', 'mp'))
Inputs may be any that keep to these rules, and one draw needn't show every extreme that they name: `segment_ids`: within each row the numbers never fall; each of the 16 numbers names 1 to 1024 tokens of the row.
All inputs are finite; a program needn't handle non-finite values.
Results may differ from a plain program's by a relative error of at most 0.0003.
Values sent between devices are 32-bit elements; how exact they have to be, the bound alone decides.
No kernel may reach another device: no remote copies, remote signals or barrier semaphores. Data moves between devices by JAX's collectives and lax.ppermute only.
A program may use at most 64 MiB of HBM per device.

v0:
```python
import jax
import jax.numpy as jnp
from jax import lax
from jax.sharding import PartitionSpec as P

EX_DEV = 16


def outer_sums(onehot, projected, width):
    inputs = projected[:, :width]
    outputs = projected[:, width:]
    weighted = onehot[:, :, None] * outputs[None, :, :]
    grads = jnp.einsum("eti,tj->eij", weighted, inputs, precision=lax.Precision.HIGHEST)
    return grads.reshape(onehot.shape[0], width * width)


def body(hidden, out_grad, proj_in, proj_out, segment_ids):
    width = proj_in.shape[0]
    examples = EX_DEV
    inputs = lax.dot_general(
        hidden, proj_in, (((1,), (1,)), ((), ())), preferred_element_type=jnp.float32
    )
    outputs = lax.dot_general(
        out_grad, proj_out, (((1,), (1,)), ((), ())), preferred_element_type=jnp.float32
    )
    projected = jnp.concatenate([inputs, outputs], axis=1)
    example_ids = segment_ids[0]
    onehot = (example_ids[None, :] == jnp.arange(examples, dtype=jnp.int32)[:, None]).astype(
        jnp.float32
    )
    counts = jnp.sum(onehot, axis=1)
    summed = lax.psum(projected, "mp")
    grads = outer_sums(onehot, summed, width)
    features = grads / jnp.sqrt(counts)[:, None]
    proj_size = width * width
    data_count = lax.axis_size("dp")
    model_count = lax.axis_size("mp")
    row_count = proj_size // (data_count * model_count)
    total_examples = examples * data_count
    col_first = (lax.axis_index("dp") * model_count + lax.axis_index("mp")) * row_count
    shard_piece = lax.all_gather(features, "dp", axis=0, tiled=True)
    left = lax.dynamic_slice_in_dim(shard_piece, col_first, row_count, 1)
    gram_rows = lax.dot_general(
        left,
        shard_piece,
        (((0,), (0,)), ((), ())),
        precision=lax.Precision.HIGHEST,
        preferred_element_type=jnp.float32,
    )
    return (features, gram_rows / total_examples)


def solution(mesh):
    placed = (P("dp", "mp"), P("dp", "mp"), P(None, "mp"), P(None, "mp"), P("dp", None))
    return jax.shard_map(
        body,
        mesh=mesh,
        in_specs=placed,
        out_specs=(P("dp", None), P(("dp", "mp"), None)),
        check_vma=False,
    )
```

profile of v0, /device:TPU:0, one launch (start us, length us, event | category | flops | bytes accessed | tf_op | source)
XLA Modules:
  0.0 124.1 jit_solution(2751535235130744079)
XLA Ops:
  7.2 0.0 copy-start
  7.2 0.0 copy-start.2
  7.2 0.0 all-reduce.2.cloned.1.call-start
  7.2 0.9 copy-done
  8.2 0.0 copy-start.1
  8.2 9.5 %fusion.8 = f32[2048,64]{0,1:T(8,128)S(1)} fusion(bf16[2048,3456]{1,0:T(8,128)(2,1)} %param.5, bf16[64,3456]{1,0:T(8,128)(2,1)S(1)} %copy-done), kind=kOutput, calls=%fused_computation.13 | convolution fusion | flops 905969664 | bytes 15122432 | tf_op jit(solution)/shard_map/dot_general | solution.py:20
  17.7 0.0 copy-done.2
  17.7 0.0 copy-done.1
  17.7 0.0 copy-start.3
  17.8 1.7 %fusion.9 = f32[2048,64]{0,1:T(8,128)S(1)} fusion(bf16[2048,1280]{1,0:T(8,128)(2,1)S(1)} %copy-done.1, bf16[64,1280]{1,0:T(8,128)(2,1)S(1)} %copy-done.2), kind=kOutput, calls=%fused_computation.14 | convolution fusion | flops 335544320 | bytes 5931008 | tf_op jit(solution)/shard_map/dot_general | solution.py:23
  19.4 1.1 pad_maximum_fusion
  20.5 0.0 all-reduce.2.cloned.1.call-update
  20.5 0.2 all-gather.2.cloned.1.call-start
  20.8 0.0 copy-done.3
  20.8 0.1 fusion.6
  20.9 54.4 %all-reduce.2.cloned.1.call-done = f32[2048,128]{0,1:T(8,128)} async-done(((f32[2048,128]{0,1:T(8,128)}), f32[2048,128]{0,1:T(8,128)}) %all-reduce.2.cloned.1.call-update) | async-done | bytes 1048592 | tf_op jit(solution)/shard_map/psum | solution.py:32
  75.4 1.1 slice.8
  76.4 7.7 %fusion = f32[16,64,64]{2,1,0:T(8,128)S(1)} fusion(f32[2048,64]{0,1:T(8,128)S(1)} %slice.8, f32[16,2048]{1,0:T(8,128)S(1)} %fusion.4, f32[2048,128]{0,1:T(8,128)} %all-reduce.2.cloned.1.call-done), kind=kOutput, calls=%fused_computation | convolution fusion | flops 1612709888 | bytes 1441792 | tf_op jit(solution)/shard_map/eti,tj->eij/dot_general | solution.py:13
  84.1 0.2 reshape.32
  84.3 0.8 broadcast_divide_fusion
  85.1 0.0 all-gather.2.cloned.1.call-update
  85.1 27.2 %all-gather.2.cloned.1.call-done = f32[128,4096]{1,0:T(8,128)} async-done(((f32[16,4096]{1,0:T(8,128)}), f32[128,4096]{1,0:T(8,128)}) %all-gather.2.cloned.1.call-update) | async-done | bytes 2097168 | tf_op jit(solution)/shard_map/all_gather | solution.py:41
  112.3 4.9 %convolution_multiply_fusion = f32[128,4096]{1,0:T(8,128)} fusion(f32[128,4096]{1,0:T(8,128)} %all-gather.2.cloned.1.call-done, s32[]{:T(128)S(6)} %select_n.3), kind=kOutput, calls=%fused_computation.2 | convolution fusion | flops 805830656 | bytes 4259844 | tf_op jit(solution)/shard_map/dot_general | solution.py:43
  (2 shorter events, 0.0 us)
Async XLA Ops:
  7.2 1.0 copy-start
  7.2 10.5 %copy-start.2 = (bf16[64,1280]{1,0:T(8,128)(2,1)S(1)}, bf16[64,1280]{1,0:T(8,128)(2,1)}, u32[]{:S(2)}) copy-start(bf16[64,1280]{1,0:T(8,128)(2,1)} %param.8) | copy-start | bytes 491524
  7.2 68.2 %all-reduce.2.cloned.1.call-start = ((), (), s32[]{:S(2)}) async-start(), calls=%async_computation | async-start | bytes 2097152 | tf_op jit(solution)/shard_map/psum | solution.py:32
  8.2 9.5 %copy-start.1 = (bf16[2048,1280]{1,0:T(8,128)(2,1)S(1)}, bf16[2048,1280]{1,0:T(8,128)(2,1)}, u32[]{:S(2)}) copy-start(bf16[2048,1280]{1,0:T(8,128)(2,1)} %param.6) | copy-start | bytes 15728644
  17.7 3.0 %copy-start.3 = (s32[1,2048]{1,0:T(1,128)S(1)}, s32[1,2048]{1,0:T(1,128)}, u32[]{:S(2)}) copy-start(s32[1,2048]{1,0:T(1,128)} %param.9) | copy-start | bytes 24580
  20.5 91.8 %all-gather.2.cloned.1.call-start = ((), (), s32[]{:S(2)}) async-start(), calls=%async_computation.1 | async-start | bytes 2359296 | tf_op jit(solution)/shard_map/all_gather | solution.py:41
Sparse Core Ops, SparseCore 0:
  20.6 54.6 all-reduce.1
  85.2 27.0 all-gather.1
where the time goes:
time: 124 us
  waiting for transfers between devices  81.7 us (66%)
  matrix products  23.8 us (19%)
  between operations  14.1 us (11%)
  local copies, waits for them, and re-layouts  2.24 us (2%)
  other arithmetic  2 us (2%)
    psum x1, waiting for transfers between devices, body(): summed = lax.psum(projected, 'mp')  54.4 us
    all_gather x1, waiting for transfers between devices, body(): shard_piece = lax.all_gather(features, 'dp', axis=0, tiled=True)  27.2 us
    dot_general x1, matrix products, body(): lax.dot_general(hidden, proj_in, (((1,), (1,)), ((), ())), preferred_elem...  9.53 us
    dot_general x1, matrix products, outer_sums(): jnp.einsum('eti,tj->eij', weighted, inputs, precision=lax.Precision.HIGHEST)  7.67 us
    dot_general x1, matrix products, body(): lax.dot_general(left, shard_piece, (((0,), (0,)), ((), ())), precision=la...  4.89 us
  transfers between devices with their start and end apart: 2, of which 2 were waited for; matrix products, arithmetic and copies ran while one was open for 0% of the time, Pallas kernels for 0%

commit v1 on v0

--- a/solution.py
+++ b/solution.py
@@ -29,7 +29,7 @@
         jnp.float32
     )
     counts = jnp.sum(onehot, axis=1)
-    summed = lax.psum(projected, "mp")
+    summed = jnp.sum(lax.all_gather(projected, "mp"), axis=0)
     grads = outer_sums(onehot, summed, width)
     features = grads / jnp.sqrt(counts)[:, None]
     proj_size = width * width

time: 124 us -> 163 us (1.31)
  waiting for transfers between devices: 81.7 us -> 110 us
  other arithmetic: 2 us -> 6.86 us
  local copies, waits for them, and re-layouts: 2.24 us -> 6.28 us
    all_gather x0 -> x1, waiting for transfers between devices: none -> 83.4 us  [body(): summed = jnp.sum(lax.all_gather(projected, 'mp'), axis=0)]
    psum x1 -> x0, waiting for transfers between devices: 54.4 us -> none  [body(): summed = lax.psum(projected, 'mp')]
    all_gather x0 -> x1, local copies, waits for them, and re-layouts: none -> 6.03 us  [body(): summed = jnp.sum(lax.all_gather(projected, 'mp'), axis=0)]
    reduce_sum x0 -> x1, other arithmetic: none -> 4.84 us  [body(): summed = jnp.sum(lax.all_gather(projected, 'mp'), axis=0)]
    dot_general x1, matrix products: 1.68 us -> 4.21 us  [body(): lax.dot_general(out_grad, proj_out, (((1,), (1,)), ((), ())), preferred_e...]
where the time goes in v1:
time: 163 us; the launch traced here: 162 us
  waiting for transfers between devices  110 us (67%)
  matrix products  25.1 us (15%)
  between operations  14.1 us (9%)
  other arithmetic  6.86 us (4%)
  local copies, waits for them, and re-layouts  6.28 us (4%)
    all_gather x1, waiting for transfers between devices, body(): summed = jnp.sum(lax.all_gather(projected, 'mp'), axis=0)  83.4 us
    all_gather x1, waiting for transfers between devices, body(): shard_piece = lax.all_gather(features, 'dp', axis=0, tiled=True)  26.4 us
    dot_general x1, matrix products, body(): lax.dot_general(hidden, proj_in, (((1,), (1,)), ((), ())), preferred_elem...  9.39 us
    dot_general x1, matrix products, outer_sums(): jnp.einsum('eti,tj->eij', weighted, inputs, precision=lax.Precision.HIGHEST)  6.63 us
    all_gather x1, local copies, waits for them, and re-layouts, body(): summed = jnp.sum(lax.all_gather(projected, 'mp'), axis=0)  6.03 us
    dot_general x1, matrix products, body(): lax.dot_general(left, shard_piece, (((0,), (0,)), ((), ())), precision=la...  4.89 us
    reduce_sum x1, other arithmetic, body(): summed = jnp.sum(lax.all_gather(projected, 'mp'), axis=0)  4.84 us
    dot_general x1, matrix products, body(): lax.dot_general(out_grad, proj_out, (((1,), (1,)), ((), ())), preferred_e...  4.21 us
  transfers between devices with their start and end apart: 2, of which 2 were waited for; matrix products, arithmetic and copies ran while one was open for 0% of the time, Pallas kernels for 0%

profile of v1, /device:TPU:0, one launch (start us, length us, event | category | flops | bytes accessed | tf_op | source)
XLA Modules:
  0.0 162.3 jit_solution(8876331291347958998)
XLA Ops:
  7.2 0.0 copy-start
  7.2 0.0 all-gather.6.cloned.1.call-start
  7.2 4.2 %fusion.9 = f32[2048,64]{0,1:T(8,128)S(1)} fusion(bf16[2048,1280]{1,0:T(8,128)(2,1)} %param.6, bf16[64,1280]{1,0:T(8,128)(2,1)} %param.8), kind=kOutput, calls=%fused_computation.14 | convolution fusion | flops 335544320 | bytes 5931008 | tf_op jit(solution)/shard_map/dot_general | solution.py:23
  11.4 0.0 copy-done
  11.5 0.0 copy-start.1
  11.5 9.4 %fusion.8 = f32[2048,64]{0,1:T(8,128)S(1)} fusion(bf16[2048,3456]{1,0:T(8,128)(2,1)} %param.5, bf16[64,3456]{1,0:T(8,128)(2,1)S(1)} %copy-done), kind=kOutput, calls=%fused_computation.13 | convolution fusion | flops 905969664 | bytes 15122432 | tf_op jit(solution)/shard_map/dot_general | solution.py:20
  20.9 1.1 pad_maximum_fusion
  21.9 0.0 all-gather.6.cloned.1.call-update
  22.0 0.0 all-gather.4.cloned.1.call-start
  22.0 0.0 copy-done.1
  22.0 0.1 fusion.6
  22.2 83.4 %all-gather.6.cloned.1.call-done = f32[8192,128]{0,1:T(8,128)} async-done(((f32[2048,128]{0,1:T(8,128)}), f32[8192,128]{0,1:T(8,128)}) %all-gather.6.cloned.1.call-update) | async-done | bytes 4194320 | tf_op jit(solution)/shard_map/all_gather | solution.py:32
  105.6 6.0 %reshape.33 = f32[4,2048,128]{1,0,2:T(4,128)} reshape(f32[8192,128]{0,1:T(8,128)} %all-gather.6.cloned.1.call-done) | data formatting | bytes 8388608 | tf_op jit(solution)/shard_map/all_gather | solution.py:32
  111.6 4.8 %reduce_sum.18 = f32[2048,128]{0,1:T(8,128)S(1)} reduce(f32[4,2048,128]{1,0,2:T(4,128)} %reshape.33, f32[]{:T(128)} %constant.4.clone.1), dimensions={0}, to_apply=%region_0.0 | reduce | flops 786432 | bytes 5242884 | tf_op jit(solution)/shard_map/reduce_sum | solution.py:32
  116.5 6.6 %fusion = f32[16,64,64]{2,1,0:T(8,128)S(1)} fusion(f32[2048,64]{0,1:T(8,128)S(1)} %slice.8, f32[16,2048]{1,0:T(8,128)S(1)} %fusion.4, f32[2048,128]{0,1:T(8,128)S(1)} %reduce_sum.18), kind=kOutput, calls=%fused_computation | convolution fusion | flops 1612709888 | bytes 1441792 | tf_op jit(solution)/shard_map/eti,tj->eij/dot_general | solution.py:13
  123.1 0.2 reshape.32
  123.3 0.8 broadcast_divide_fusion
  124.1 0.0 all-gather.4.cloned.1.call-update
  124.1 26.4 %all-gather.4.cloned.1.call-done = f32[128,4096]{1,0:T(8,128)} async-done(((f32[16,4096]{1,0:T(8,128)}), f32[128,4096]{1,0:T(8,128)}) %all-gather.4.cloned.1.call-update) | async-done | bytes 2097168 | tf_op jit(solution)/shard_map/all_gather | solution.py:41
  150.6 4.9 %convolution_multiply_fusion = f32[128,4096]{1,0:T(8,128)} fusion(f32[128,4096]{1,0:T(8,128)} %all-gather.4.cloned.1.call-done, s32[]{:T(128)S(6)} %select_n.3), kind=kOutput, calls=%fused_computation.2 | convolution fusion | flops 805830656 | bytes 4259844 | tf_op jit(solution)/shard_map/dot_general | solution.py:43
  (3 shorter events, 0.1 us)
Async XLA Ops:
  7.2 4.3 %copy-start = (bf16[64,3456]{1,0:T(8,128)(2,1)S(1)}, bf16[64,3456]{1,0:T(8,128)(2,1)}, u32[]{:S(2)}) copy-start(bf16[64,3456]{1,0:T(8,128)(2,1)} %param.7) | copy-start | bytes 1327108
  7.2 98.4 %all-gather.6.cloned.1.call-start = ((), (), s32[]{:S(2)}) async-start(), calls=%async_computation.1 | async-start | bytes 5242880 | tf_op jit(solution)/shard_map/all_gather | solution.py:32
  11.5 10.6 %copy-start.1 = (s32[1,2048]{1,0:T(1,128)S(1)}, s32[1,2048]{1,0:T(1,128)}, u32[]{:S(2)}) copy-start(s32[1,2048]{1,0:T(1,128)} %param.9) | copy-start | bytes 24580
  22.0 128.6 %all-gather.4.cloned.1.call-start = ((), (), s32[]{:S(2)}) async-start(), calls=%async_computation | async-start | bytes 2359296 | tf_op jit(solution)/shard_map/all_gather | solution.py:41
Sparse Core Ops, SparseCore 0:
  22.1 83.4 all-gather.5
  124.3 26.2 all-gather.3
